TPU v7x, 16 devices: a 4x2x1 block of a 4x4x4 slice. The times are simulated.
16 devices in a mesh: dp: 2 (over y, z), tp: 8 (over x, core).
Axes of the slice: x: 4, y: 2, z: 1, core: 2. Of those that a mesh axis runs over, the one named last changes fastest.
The devices are a block of a 4x4x4 slice.
Arguments:
- x: bfloat16 [128, 3584], P('dp'), parts along dimension 0
- k_cache: bfloat16 [128, 4096, 8, 256], P('dp', None, 'tp'), parts along dimension 0
- v_cache: bfloat16 [128, 4096, 8, 256], P('dp', None, 'tp'), parts along dimension 0
- gain_a: bfloat16 [3584], replicated
- wq: bfloat16 [3584, 4096], P(None, 'tp')
- wo: bfloat16 [4096, 3584], P('tp')
- gain_m: bfloat16 [3584], replicated
- w_gate: bfloat16 [3584, 14336], P(None, 'tp')
- w_up: bfloat16 [3584, 14336], P(None, 'tp')
- w_down: bfloat16 [14336, 3584], P('tp')
Outputs:
- output: bfloat16 [128, 3584], P('dp'), parts along dimension 0
There are 2 independent parts. A program takes and returns all parts, laid end to end along the dimension named above; an argument that names none is the same for every part.
All inputs are finite; a program needn't handle non-finite values.
Results may differ from a plain program's by a relative error of at most 0.017.
Values are sent between devices in bfloat16 or wider.
A program may use at most 1.5 GiB of HBM per device.

v0:
```python
import jax
import jax.numpy as jnp
from jax import lax
from jax.sharding import PartitionSpec as P

HEAD = 256
THETA = 10000


def normed(x, gain):
    wide = x.astype(jnp.float32)
    scale = lax.rsqrt(jnp.mean(wide * wide, -1, keepdims=True) + 1e-6)
    return (wide * scale * gain.astype(jnp.float32)).astype(jnp.bfloat16)


def turned(t, place, theta):
    half = t.shape[-1] // 2
    angle = place.astype(jnp.float32)[:, None] * theta ** (-jnp.arange(half, dtype=jnp.float32) / half)
    cos, sin = jnp.cos(angle)[:, None], jnp.sin(angle)[:, None]
    a, b = t[..., :half].astype(jnp.float32), t[..., half:].astype(jnp.float32)
    return jnp.concatenate([a * cos - b * sin, b * cos + a * sin], -1).astype(jnp.bfloat16)


def matmul(a, w):
    return jnp.dot(a, w, preferred_element_type=jnp.float32).astype(jnp.bfloat16)


def einsum(form, a, b):
    return jnp.einsum(form, a.astype(jnp.float32), b.astype(jnp.float32))


def seen_by(a, wq, k_cache, v_cache, head, theta):
    batch, cache, kv_heads = k_cache.shape[:3]
    place = jnp.full((batch,), cache - 1)
    q = turned(matmul(a, wq).reshape(batch, -1, head), place, theta).reshape(batch, kv_heads, -1, head)
    scores = einsum("bgsd,bugd->bgsu", q, k_cache) * head**-0.5
    weights = jax.nn.softmax(scores, -1).astype(jnp.bfloat16)
    return einsum("bgsu,bugd->bgsd", weights, v_cache).astype(jnp.bfloat16).reshape(batch, -1)


def hidden_of(b, w_gate, w_up):
    gate = jnp.dot(b, w_gate, preferred_element_type=jnp.float32)
    up = jnp.dot(b, w_up, preferred_element_type=jnp.float32)
    return (jax.nn.silu(gate) * up).astype(jnp.bfloat16)


def solution(mesh):
    def added(t, term):
        return (t.astype(jnp.float32) + lax.psum(term.astype(jnp.bfloat16), "tp").astype(jnp.float32)).astype(jnp.bfloat16)

    def step(x, k_cache, v_cache, gain_a, wq, wo, gain_m, w_gate, w_up, w_down):
        seen = seen_by(normed(x, gain_a), wq, k_cache, v_cache, HEAD, THETA)
        h = added(x, jnp.dot(seen, wo, preferred_element_type=jnp.float32))
        return added(h, jnp.dot(hidden_of(normed(h, gain_m), w_gate, w_up), w_down, preferred_element_type=jnp.float32))

    states, cache, columns, rows_of = P("dp", None), P("dp", None, "tp", None), P(None, "tp"), P("tp", None)
    return jax.shard_map(
        step,
        mesh=mesh,
        in_specs=(states, cache, cache, P(None), columns, rows_of, P(None), columns, columns, rows_of),
        out_specs=states,
        check_vma=False,
    )
```

profile of v0, /device:TPU:113, one launch (start us, length us, event | category | flops | bytes accessed | tf_op | source)
XLA Modules:
  0.0 243.8 jit_solution(7020237294641413698)
XLA Ops:
  6.5 0.0 all-reduce.3.cloned.1.call-start
  6.6 0.7 convert_element_type.66
  7.3 1.2 fusion.15
  8.5 3.0 %convolution_convert_fusion.2 = bf16[64,512]{1,0:T(8,128)(2,1)S(1)} fusion(bf16[3584,512]{1,0:T(8,128)(2,1)} %param.14, bf16[64,3584]{1,0:T(8,128)(2,1)} %param.10, f32[3584]{0:T(1024)S(1)} %convert_element_type.66, f32[64]{0:T(128)S(1)} %add_rsqrt_fusion.1), kind=kOutput, calls=%fused_computation.20 | convolution fusion | flops 235831296 | bytes 4208896 | tf_op jit(solution)/shard_map/dot_general | solution.py:25
  11.7 47.3 %fusion.7 = f32[64,2,4096]{2,1,0:T(2,128)S(1)} fusion(bf16[64,4096,1,256]{3,1,2,0:T(8,128)(2,1)} %param.11, bf16[64,2,256]{2,0,1:T(8,128)(2,1)S(1)} %pad_maximum_fusion), kind=kOutput, calls=%fused_computation.7 | convolution fusion | flops 268959744 | bytes 136380416 | tf_op jit(solution)/shard_map/bgsd,bugd->bgsu/dot_general | solution.py:29
  59.0 1.8 fusion.46
  60.8 43.1 %fusion.11 = bf16[64,2,256]{2,1,0:T(2,128)(2,1)S(1)} fusion(bf16[64,4096,1,256]{3,1,2,0:T(8,128)(2,1)} %param.12, f32[64,2]{1,0:T(8,128)S(1)} %fusion.46, f32[64,2,4096]{2,1,0:T(2,128)S(1)} %fusion.7), kind=kOutput, calls=%fused_computation.19 | convolution fusion | flops 270045312 | bytes 136380928 | tf_op jit(solution)/shard_map/bgsu,bugd->bgsd/dot_general | solution.py:29
  103.9 0.0 copy-start.1
  103.9 0.0 copy-start
  103.9 3.6 %convolution_convert_fusion.1 = bf16[64,3584]{1,0:T(8,128)(2,1)} fusion(bf16[64,512]{1,0:T(8,128)(2,1)S(1)} %bitcast.24, bf16[512,3584]{1,0:T(8,128)(2,1)} %param.15), kind=kOutput, calls=%fused_computation.9 | convolution fusion | flops 235110400 | bytes 4194304 | tf_op jit(solution)/shard_map/dot_general | solution.py:53
  107.5 0.1 all-reduce.3.cloned.1.call-update
  107.6 0.2 all-reduce.5.cloned.1.call-start
  107.8 0.0 copy-done.1
  107.8 53.3 %all-reduce.3.cloned.1.call-done = bf16[64,3584]{1,0:T(8,128)(2,1)} async-done(((bf16[64,3584]{1,0:T(8,128)(2,1)}), bf16[64,3584]{1,0:T(8,128)(2,1)}) %all-reduce.3.cloned.1.call-update) | async-done | bytes 458768 | tf_op jit(solution)/shard_map/psum | solution.py:49
  161.1 0.0 copy-done
  161.2 1.3 fusion.19
  162.4 7.1 %fusion.34 = f32[64,1792]{1,0:T(8,128)S(1)} fusion(bf16[3584,1792]{1,0:T(8,128)(2,1)} %param.17, bf16[64,3584]{1,0:T(8,128)(2,1)S(1)} %get-tuple-element.6, f32[3584]{0:T(1024)S(1)} %convert_element_type.77, f32[64]{0:T(128)S(1)} %add_rsqrt_fusion), kind=kOutput, calls=%fused_computation.38 | convolution fusion | flops 823001088 | bytes 13777152 | tf_op jit(solution)/shard_map/dot_general | solution.py:42
  169.5 13.6 %convolution_convert_fusion = bf16[64,3584]{1,0:T(8,128)(2,1)} fusion(bf16[1792,3584]{1,0:T(8,128)(2,1)} %param.19, bf16[3584,1792]{1,0:T(8,128)(2,1)} %param.18, f32[64,1792]{1,0:T(8,128)S(1)} %fusion.34, bf16[64,3584]{1,0:T(8,128)(2,1)S(1)} %get-tuple-element.6, f32[3584]{0:T(1024)S(1)} %convert_element_type.77, f32[64]{0:T(128)S(1)} %add_rsqrt_fusion), kind=kOutput, calls=%fused_computation.8 | convolution fusion | flops 1646002176 | bytes 27080960 | tf_op jit(solution)/shard_map/dot_general | solution.py:54
  183.1 0.1 all-reduce.5.cloned.1.call-update
  183.1 51.9 %all-reduce.5.cloned.1.call-done = bf16[64,3584]{1,0:T(8,128)(2,1)} async-done(((bf16[64,3584]{1,0:T(8,128)(2,1)}), bf16[64,3584]{1,0:T(8,128)(2,1)}) %all-reduce.5.cloned.1.call-update) | async-done | bytes 458768 | tf_op jit(solution)/shard_map/psum | solution.py:49
  235.0 1.9 fusion.22
  (9 shorter events, 0.2 us)
Async XLA Ops:
  6.5 154.6 %all-reduce.3.cloned.1.call-start = ((), (), s32[]{:S(2)}) async-start(), calls=%async_computation | async-start | bytes 917504 | tf_op jit(solution)/shard_map/psum | solution.py:49
  103.9 4.0 %copy-start.1 = (bf16[3584]{0:T(1024)(128)(2,1)S(1)}, bf16[3584]{0:T(1024)(128)(2,1)}, u32[]{:S(2)}) copy-start(bf16[3584]{0:T(1024)(128)(2,1)} %param.16) | copy-start | bytes 21508
  103.9 57.3 %copy-start = (bf16[64,3584]{1,0:T(8,128)(2,1)S(1)}, bf16[64,3584]{1,0:T(8,128)(2,1)}, u32[]{:S(2)}) copy-start(bf16[64,3584]{1,0:T(8,128)(2,1)} %param.10) | copy-start | bytes 1376260
  107.6 127.5 %all-reduce.5.cloned.1.call-start = ((), (), s32[]{:S(2)}) async-start(), calls=%async_computation.1 | async-start | bytes 917504 | tf_op jit(solution)/shard_map/psum | solution.py:49
Sparse Core Ops, SparseCore 0:
  107.7 53.4 all-reduce.2
  183.3 51.7 all-reduce.4
where the time goes:
time: 246 us; the launch traced here: 244 us
  matrix products  118 us (48%)
  waiting for transfers between devices  105 us (43%)
  between operations  13.5 us (5%)
  other arithmetic  6.99 us (3%)
    psum x2, waiting for transfers between devices, added(): lax.psum(term.astype(jnp.bfloat16), 'tp').astype(jnp.float32)  105 us
    dot_general x2, matrix products, einsum(): return jnp.einsum(form, a.astype(jnp.float32), b.astype(jnp.float32))  90.4 us
    dot_general x1, matrix products, step(): jnp.dot(hidden_of(normed(h, gain_m), w_gate, w_up), w_down, preferred_ele...  13.6 us
    dot_general x1, matrix products, hidden_of(): gate = jnp.dot(b, w_gate, preferred_element_type=jnp.float32)  7.06 us
  transfers between devices with their start and end apart: 2, of which 2 were waited for; matrix products, arithmetic and copies ran while one was open for 0% of the time, Pallas kernels for 0%

commit v1 on v0

v1 whole, which is shorter than its diff:
```python
import functools

import jax
import jax.numpy as jnp
from jax import lax
from jax.experimental import pallas as pl
from jax.experimental.pallas import tpu as pltpu
from jax.sharding import PartitionSpec as P

HEAD = 256
THETA = 10000
SLOTS = 3
SPLIT = 2
HIDDEN_TILE = 256
OUT_TILE = 512
VMEM_LIMIT = 67_043_328
F32 = jnp.float32
BF16 = jnp.bfloat16


def rem(a, b):
    return a % b if isinstance(a, int) else lax.rem(a, b)


def tile_at(i, size):
    return pl.ds(i * size if isinstance(i, int) else pl.multiple_of(i * size, size), size)


def normed(wide, gain):
    scale = lax.rsqrt(jnp.mean(wide * wide, -1, keepdims=True) + 1e-6)
    return wide * scale * gain


def layer(
    n,
    x_ref, k_ref, v_ref, ga_ref, wq_ref, wo_ref, gm_ref, wg_ref, wu_ref, wd_ref, cs_ref,
    y_ref,
    xv, gav, gmv, csv, ks, vs, wov, wgv, wuv, wdv, qf, scores, seen, terms, hf, bf, b16, hid, outf, out16, sums, yown,
    in_sem, k_sem, v_sem, wq_sem, wo_sem, g_sem, u_sem, d_sem,
    t_send, t_recv, s_send, s_recv, y_send, y_recv, own_sem,
):
    me = lax.axis_index("tp")
    rows, d = xv.shape
    cache, head = ks.shape[1:]
    heads = wq_ref.shape[1] // head
    half = head // 2
    block = terms.shape[2]
    ng, nd = wgv.shape[0], wdv.shape[0]
    gt, dt = wgv.shape[2], wdv.shape[2]

    def peer(j):
        return rem(me + j, n)

    def at(dev):
        return {"tp": dev}

    def kv_start(hbm, slots, sem, s, slot):
        part = cache // SPLIT
        for i in range(SPLIT):
            pltpu.make_async_copy(hbm.at[s, pl.ds(i * part, part)], slots.at[slot, pl.ds(i * part, part)], sem.at[slot]).start()

    def kv_wait(hbm, slots, sem, slot):
        pltpu.make_async_copy(hbm.at[0], slots.at[slot], sem.at[slot]).wait()

    def start_k(s):
        kv_start(k_ref, ks, k_sem, s, rem(s, SLOTS))

    def start_v(s):
        kv_start(v_ref, vs, v_sem, s, rem(s, SLOTS))

    small = [(x_ref, xv), (ga_ref, gav), (gm_ref, gmv), (cs_ref, csv)]
    small = [pltpu.make_async_copy(a, b, in_sem.at[i]) for i, (a, b) in enumerate(small)]
    wq_into = [ks.at[SLOTS - 1, pl.ds(0, d)], vs.at[SLOTS - 1, pl.ds(0, d)]]
    wq_in = [pltpu.make_async_copy(wq_ref.at[:, pl.ds(i * head, head)], wq_into[i], wq_sem.at[i]) for i in range(heads)]
    wo_in = pltpu.make_async_copy(wo_ref, wov, wo_sem)
    gate_in = [pltpu.make_async_copy(wg_ref.at[:, pl.ds(j * gt, gt)], wgv.at[j], g_sem.at[j]) for j in range(ng)]
    up_in = [pltpu.make_async_copy(wu_ref.at[:, pl.ds(j * gt, gt)], wuv.at[j], u_sem.at[j]) for j in range(ng)]
    down_in = [pltpu.make_async_copy(wd_ref.at[:, pl.ds(j * dt, dt)], wdv.at[j], d_sem.at[j]) for j in range(nd)]
    weights_in = [c for pair in zip(gate_in, up_in) for c in pair] + down_in

    for c in small + wq_in:
        c.start()
    for s in range(SLOTS - 1):
        kv_start(k_ref, ks, k_sem, s, s)
        kv_start(v_ref, vs, v_sem, s, s)
    wo_in.start()

    barrier = pltpu.get_barrier_semaphore()
    for j in range(1, n):
        pl.semaphore_signal(barrier, inc=1, device_id=at(peer(j)), device_id_type=pl.DeviceIdType.MESH)

    for c in small:
        c.wait()
    a = normed(xv[...].astype(F32), gav[...].astype(F32)).astype(BF16)
    cos, sin = csv[0:1], csv[1:2]
    for i in range(heads):
        wq_in[i].wait()
        q = jnp.dot(a, wq_into[i][...], preferred_element_type=F32).astype(BF16).astype(F32)
        lo, hi = q[:, :half], q[:, half:]
        qf[:, i * head : i * head + half] = (lo * cos - hi * sin).astype(BF16).astype(F32)
        qf[:, i * head + half : (i + 1) * head] = (hi * cos + lo * sin).astype(BF16).astype(F32)
    kv_start(k_ref, ks, k_sem, SLOTS - 1, SLOTS - 1)
    kv_start(v_ref, vs, v_sem, SLOTS - 1, SLOTS - 1)
    pl.semaphore_wait(barrier, n - 1)

    def score(s):
        slot = rem(s, SLOTS)
        row = qf[pl.ds(s, 1), :]
        which = lax.broadcasted_iota(jnp.int32, (8, head), 0)
        q = jnp.zeros((8, head), F32)
        for i in range(heads):
            q = jnp.where(which == i, row[:, i * head : (i + 1) * head], q)
        scores[rem(s, 2)] = lax.dot_general(q.astype(BF16), ks[slot], (((1,), (1,)), ((), ())), preferred_element_type=F32)

    def attend(s):
        sc = scores[rem(s, 2)]
        e = jnp.exp((sc - jnp.max(sc, -1, keepdims=True)) * head**-0.5)
        p = (e * (1.0 / jnp.sum(e, -1, keepdims=True))).astype(BF16)
        slot = rem(s, SLOTS)
        hc = cache // 2
        o = jnp.dot(p[:, :hc], vs[slot, :hc], preferred_element_type=F32)
        o = o + jnp.dot(p[:, hc:], vs[slot, hc:], preferred_element_type=F32)
        r = rem(s, block)
        for i in range(heads):
            seen[pl.ds(r, 1), i * head : (i + 1) * head] = o[i : i + 1]

    def term_copy(c, j):
        return pltpu.make_async_remote_copy(
            src_ref=terms.at[0, c],
            dst_ref=terms.at[j, c],
            send_sem=t_send.at[c, j],
            recv_sem=t_recv.at[c, j],
            device_id=at(peer(j)),
            device_id_type=pl.DeviceIdType.MESH,
        )

    def send_terms(c):
        terms[0, c] = jnp.dot(seen[...].astype(BF16), wov[...], preferred_element_type=F32).astype(BF16)
        for j in range(1, n):
            term_copy(c, j).start()

    def take_terms(c):
        for j in range(1, n):
            term_copy(c, j).wait_recv()
        at_rows = tile_at(c, block)
        total = terms[rem(me + n, n), c].astype(F32)
        for r in range(1, n):
            total = total + terms[rem(me - r + n, n), c].astype(F32)
        h = (hf[at_rows, :] + total).astype(BF16).astype(F32)
        hf[at_rows, :] = h
        bf[at_rows, :] = normed(h, gmv[...].astype(F32))

    hf[...] = xv[...].astype(F32)
    kv_wait(k_ref, ks, k_sem, 0)
    score(0)
    first_spare = rows - 1 - SLOTS

    def step(s, _):
        kv_wait(k_ref, ks, k_sem, rem(s + 1, SLOTS))
        kv_wait(v_ref, vs, v_sem, rem(s, SLOTS))
        score(s + 1)
        attend(s)

        @pl.when(s + 1 + SLOTS < rows)
        def _():
            start_k(s + 1 + SLOTS)

        @pl.when(s + SLOTS < rows)
        def _():
            start_v(s + SLOTS)

        for i in range(SLOTS):

            @pl.when(s == first_spare + i)
            def _():
                for c in weights_in[i * 3 : i * 3 + 3]:
                    c.start()

        @pl.when(rem(s, block) == block - 1)
        def _():
            c = s // block

            @pl.when(c == 0)
            def _():
                wo_in.wait()

            send_terms(c)

            @pl.when(c > 0)
            def _():
                take_terms(c - 1)

        return 0

    start_k(SLOTS)
    lax.fori_loop(0, rows - 1, step, 0)
    for c in weights_in[3 * SLOTS :]:
        c.start()
    kv_wait(v_ref, vs, v_sem, (rows - 1) % SLOTS)
    attend(rows - 1)
    last = rows // block - 1
    send_terms(last)
    take_terms(last - 1)
    take_terms(last)

    b16[...] = bf[...].astype(BF16)

    def hidden(j, _):
        pltpu.make_async_copy(wg_ref.at[:, pl.ds(0, gt)], wgv.at[j], g_sem.at[j]).wait()
        pltpu.make_async_copy(wu_ref.at[:, pl.ds(0, gt)], wuv.at[j], u_sem.at[j]).wait()
        gate = jnp.dot(b16[...], wgv[j], preferred_element_type=F32)
        up = jnp.dot(b16[...], wuv[j], preferred_element_type=F32)
        hid[:, tile_at(j, gt)] = (jax.nn.silu(gate) * up).astype(BF16)
        return 0

    lax.fori_loop(0, ng, hidden, 0)

    my_rows = tile_at(me, block)

    def sum_copy(t, j):
        return pltpu.make_async_remote_copy(
            src_ref=out16.at[t, peer(j)],
            dst_ref=sums.at[j, t],
            send_sem=s_send.at[t, j],
            recv_sem=s_recv.at[t, j],
            device_id=at(peer(j)),
            device_id_type=pl.DeviceIdType.MESH,
        )

    def y_at(t, dev):
        return y_ref.at[tile_at(dev, block), tile_at(t, dt)]

    def y_copy(t, j):
        return pltpu.make_async_remote_copy(
            src_ref=yown.at[t],
            dst_ref=y_at(t, me),
            send_sem=y_send.at[t, j],
            recv_sem=y_recv.at[t, j],
            device_id=at(peer(j)),
            device_id_type=pl.DeviceIdType.MESH,
        )

    def y_local(t):
        return pltpu.make_async_copy(yown.at[t], y_at(t, me), own_sem.at[t])

    def finish(t):
        for j in range(1, n):
            sum_copy(t, j).wait_recv()
        total = outf[t, my_rows, :]
        for j in range(1, n):
            total = total + sums[j, t].astype(F32)
        yown[t] = (hf[my_rows, tile_at(t, dt)] + total).astype(BF16)
        for j in range(1, n):
            y_copy(t, j).start()
        y_local(t).start()

    def down(t, _):
        pltpu.make_async_copy(wd_ref.at[:, pl.ds(0, dt)], wdv.at[t], d_sem.at[t]).wait()
        out = jnp.dot(hid[...], wdv[t], preferred_element_type=F32)
        outf[t] = out
        out16[t] = out.reshape(n, block, dt).astype(BF16)
        for j in range(1, n):
            sum_copy(t, j).start()

        @pl.when(t > 1)
        def _():
            finish(t - 2)

        return 0

    lax.fori_loop(0, nd, down, 0)
    finish(nd - 2)
    finish(nd - 1)

    def drain_y(t, _):
        for j in range(1, n):
            sum_copy(t, j).wait_send()
            y_copy(t, j).wait_send()
            y_copy(t, j).wait_recv()
        y_local(t).wait()
        return 0

    def drain_t(c, _):
        for j in range(1, n):
            term_copy(c, j).wait_send()
        return 0

    lax.fori_loop(0, last + 1, drain_t, 0)
    lax.fori_loop(0, nd, drain_y, 0)


def solution(mesh):
    n = mesh.shape["tp"]

    def step(x, k_cache, v_cache, gain_a, wq, wo, gain_m, w_gate, w_up, w_down):
        rows, d = x.shape
        cache, _, head = k_cache.shape[1:]
        half = head // 2
        angle = F32(cache - 1) * THETA ** (-jnp.arange(half, dtype=F32) / half)
        turn = jnp.stack([jnp.cos(angle), jnp.sin(angle)])
        block = rows // n
        chunks = rows // block
        ff = w_gate.shape[1]
        ng, nd = ff // HIDDEN_TILE, d // OUT_TILE
        k, v = (c.reshape(rows, cache, head) for c in (k_cache, v_cache))
        dma = pltpu.SemaphoreType.DMA
        return pl.pallas_call(
            functools.partial(layer, n),
            out_shape=jax.ShapeDtypeStruct((rows, d), BF16),
            in_specs=[pl.BlockSpec(memory_space=pl.ANY)] * 11,
            out_specs=pl.BlockSpec(memory_space=pl.ANY),
            scratch_shapes=[
                pltpu.VMEM((rows, d), BF16),
                pltpu.VMEM((1, d), BF16),
                pltpu.VMEM((1, d), BF16),
                pltpu.VMEM((2, half), F32),
                pltpu.VMEM((SLOTS, cache, head), BF16),
                pltpu.VMEM((SLOTS, cache, head), BF16),
                pltpu.VMEM(wo.shape, BF16),
                pltpu.VMEM((ng, d, HIDDEN_TILE), BF16),
                pltpu.VMEM((ng, d, HIDDEN_TILE), BF16),
                pltpu.VMEM((nd, ff, OUT_TILE), BF16),
                pltpu.VMEM((rows, wq.shape[1]), F32),
                pltpu.VMEM((2, 8, cache), F32),
                pltpu.VMEM((block, wq.shape[1]), F32),
                pltpu.VMEM((n, chunks, block, d), BF16),
                pltpu.VMEM((rows, d), F32),
                pltpu.VMEM((rows, d), F32),
                pltpu.VMEM((rows, d), BF16),
                pltpu.VMEM((rows, ff), BF16),
                pltpu.VMEM((nd, rows, OUT_TILE), F32),
                pltpu.VMEM((nd, n, block, OUT_TILE), BF16),
                pltpu.VMEM((n, nd, block, OUT_TILE), BF16),
                pltpu.VMEM((nd, block, OUT_TILE), BF16),
                dma((4,)),
                dma((SLOTS,)),
                dma((SLOTS,)),
                dma((2,)),
                dma,
                dma((ng,)),
                dma((ng,)),
                dma((nd,)),
                dma((chunks, n)),
                dma((chunks, n)),
                dma((nd, n)),
                dma((nd, n)),
                dma((nd, n)),
                dma((nd, n)),
                dma((nd,)),
            ],
            compiler_params=pltpu.CompilerParams(collective_id=0, has_side_effects=True, vmem_limit_bytes=VMEM_LIMIT),
        )(x, k, v, gain_a.reshape(1, d), wq, wo, gain_m.reshape(1, d), w_gate, w_up, w_down, turn)

    states, cache, columns, rows_of = P("dp", None), P("dp", None, "tp", None), P(None, "tp"), P("tp", None)
    return jax.shard_map(
        step,
        mesh=mesh,
        in_specs=(states, cache, cache, P(None), columns, rows_of, P(None), columns, columns, rows_of),
        out_specs=states,
        check_vma=False,
    )
```

time: 246 us -> 166 us (0.67)
  Pallas kernels: 0 us -> 160 us
  matrix products: 118 us -> 0 us
  waiting for transfers between devices: 105 us -> 0 us
  between operations: 13.5 us -> 0.01 us
  other arithmetic: 6.99 us -> 0.63 us
  local copies, waits for them, and re-layouts: 0.09 us -> 4.42 us
    pallas_call x0 -> x1, Pallas kernels: none -> 160 us  [step(): pl.pallas_call(functools.partial(layer, n), out_shape=jax.ShapeDtypeStruc...]
    dot_general x6 -> x0, matrix products: 118 us -> none  [the longest x2 90.4 us: einsum(): return jnp.einsum(form, a.astype(jnp.float32), b.astype(jnp.float32))]
    psum x2 -> x0, waiting for transfers between devices: 105 us -> none  [added(): lax.psum(term.astype(jnp.bfloat16), 'tp').astype(jnp.float32)]
    convert_element_type x3 -> x0, other arithmetic: 2.6 us -> none  [the longest x1 1.89 us: added(): (t.astype(jnp.float32) + lax.psum(term.astype(jnp.bfloat16), 'tp').astype...]
    reshape x1 -> x2, local copies, waits for them, and re-layouts: 0.02 us -> 2.61 us  [the longest x1 1.3 us: step(): gain_a.reshape(1, d)]
    reduce_sum x2 -> x0, other arithmetic: 2.49 us -> none  [normed(): scale = lax.rsqrt(jnp.mean(wide * wide, -1, keepdims=True) + 1e-06)]
  transfers between devices with their start and end apart: 2 -> 0, of which waited for: 2 -> 0; matrix products, arithmetic and copies ran while one was open for 0% -> 0% of each run, Pallas kernels for 0% -> 0%
where the time goes in v1:
time: 166 us; the launch traced here: 165 us
  Pallas kernels  160 us (96%)
  local copies, waits for them, and re-layouts  4.42 us (3%)
    pallas_call x1, Pallas kernels, step(): pl.pallas_call(functools.partial(layer, n), out_shape=jax.ShapeDtypeStruc...  160 us

profile of v1, /device:TPU:113, one launch (start us, length us, event | category | flops | bytes accessed | tf_op | source)
XLA Modules:
  0.0 165.3 jit_solution(5716686633741363421)
XLA Ops:
  0.0 0.1 fusion
  0.1 0.6 pad_maximum_fusion.cs_ref
  0.6 1.3 reshape.37.ga_ref
  1.9 1.3 reshape.38.gm_ref
  3.2 160.3 %shard_map.100 = bf16[64,3584]{1,0:T(8,128)(2,1)} custom-call(bf16[64,3584]{1,0:T(8,128)(2,1)} %x_ref.1, bf16[64,4096,256]{2,1,0:T(8,128)(2,1)} %bitcast.k_ref, bf16[64,4096,256]{2,1,0:T(8,128)(2,1)} %bitcast.1.v_ref, bf16[1,3584]{1,0:T(2,128)(2,1)} %reshape.37.ga_ref, bf16[3584,512]{1,0:T(8,128)(2,1)} %wq_ref.1, bf16[512,3584]{1,0:T(8,128)(2,1)} %wo_ref.1, ...), custom_call_target="tpu_custom_call" | custom-call | tf_op jit(solution)/shard_map/pallas_call | solution.py:307
  163.5 1.8 %copy.12 = bf16[64,3584]{1,0:T(8,128)(2,1)} copy(bf16[64,3584]{1,0:T(8,128)(2,1)} %shard_map.100) | data formatting | bytes 917504

commit v2 on v1

v2 whole, which is shorter than its diff:
```python
import functools

import jax
import jax.numpy as jnp
from jax import lax
from jax.experimental import pallas as pl
from jax.experimental.pallas import tpu as pltpu
from jax.sharding import PartitionSpec as P

HEAD = 256
THETA = 10000
SLOTS = 3
SPLIT = 2
HIDDEN_TILE = 256
OUT_TILE = 512
FEW = 4
LAG = 4
VMEM_LIMIT = 66_000_000
F32 = jnp.float32
BF16 = jnp.bfloat16


def rem(a, b):
    return a % b if isinstance(a, int) else lax.rem(a, b)


def tile_at(i, size):
    return pl.ds(i * size if isinstance(i, int) else pl.multiple_of(i * size, size), size)


def normed(wide, gain):
    scale = lax.rsqrt(jnp.mean(wide * wide, -1, keepdims=True) + 1e-6)
    return wide * scale * gain


def layer(
    n,
    x_ref, k_ref, v_ref, ga_ref, wq_ref, wo_ref, gm_ref, wg_ref, wu_ref, wd_ref, cos_ref, sin_ref,
    y_ref,
    xv, gav, gmv, cosv, sinv, ks, vs, wov, wgv, wuv, wdv, qf, scores, probs, seen, terms, hf, bf, b16, hid, outf, out16, pair, mid, sums,
    in_sem, k_sem, v_sem, wq_sem, wo_sem, g_sem, u_sem, d_sem,
    t_send, t_recv, a_send, a_recv, m_send, m_recv, y_send, y_recv, f_send, f_recv,
):
    me = lax.axis_index("tp")
    rows, d = xv.shape
    cache, head = ks.shape[1:]
    heads = wq_ref.shape[1] // head
    half = head // 2
    few = terms.shape[2]
    block = rows // n
    group = block // few
    ng, nd = wgv.shape[0], wdv.shape[0]
    gt, dt = wgv.shape[2], wdv.shape[2]
    chips = n // 2
    core, chip = lax.rem(me, 2), me // 2
    partner = me + 1 - 2 * core

    def peer(j):
        return lax.rem(me + j, n)

    def chip_at(j):
        return lax.rem(chip + j, chips)

    def remote(src, dst, send, recv, dev):
        return pltpu.make_async_remote_copy(
            src_ref=src, dst_ref=dst, send_sem=send, recv_sem=recv, device_id={"tp": dev}, device_id_type=pl.DeviceIdType.MESH
        )

    def kv_start(hbm, slots, sem, s, slot):
        part = cache // SPLIT
        for i in range(SPLIT):
            pltpu.make_async_copy(hbm.at[s, pl.ds(i * part, part)], slots.at[slot, pl.ds(i * part, part)], sem.at[slot]).start()

    def kv_wait(hbm, slots, sem, slot):
        pltpu.make_async_copy(hbm.at[0], slots.at[slot], sem.at[slot]).wait()

    def start_k(s):
        kv_start(k_ref, ks, k_sem, s, rem(s, SLOTS))

    def start_v(s):
        kv_start(v_ref, vs, v_sem, s, rem(s, SLOTS))

    small = [(x_ref, xv), (ga_ref, gav), (gm_ref, gmv), (cos_ref, cosv), (sin_ref, sinv)]
    small = [pltpu.make_async_copy(a, b, in_sem.at[i]) for i, (a, b) in enumerate(small)]
    wq_into = [ks.at[SLOTS - 1, pl.ds(0, d)], vs.at[SLOTS - 1, pl.ds(0, d)]]
    wq_in = [pltpu.make_async_copy(wq_ref.at[:, pl.ds(i * head, head)], wq_into[i], wq_sem.at[i]) for i in range(heads)]
    wo_in = pltpu.make_async_copy(wo_ref, wov, wo_sem)
    gate_in = [pltpu.make_async_copy(wg_ref.at[:, pl.ds(j * gt, gt)], wgv.at[j], g_sem.at[j]) for j in range(ng)]
    up_in = [pltpu.make_async_copy(wu_ref.at[:, pl.ds(j * gt, gt)], wuv.at[j], u_sem.at[j]) for j in range(ng)]
    down_in = [pltpu.make_async_copy(wd_ref.at[:, pl.ds(j * dt, dt)], wdv.at[j], d_sem.at[j]) for j in range(nd)]
    weights_in = [c for two in zip(gate_in, up_in) for c in two] + down_in

    for c in small + wq_in:
        c.start()
    for s in range(SLOTS - 1):
        start_k(s)
        start_v(s)
    wo_in.start()

    barrier = pltpu.get_barrier_semaphore()
    for j in range(1, n):
        pl.semaphore_signal(barrier, inc=1, device_id={"tp": peer(j)}, device_id_type=pl.DeviceIdType.MESH)

    for c in small:
        c.wait()
    a = normed(xv[...].astype(F32), gav[...].astype(F32).reshape(1, d)).astype(BF16)
    cos, sin = cosv[...], sinv[...]
    for i in range(heads):
        wq_in[i].wait()
        q = jnp.dot(a, wq_into[i][...], preferred_element_type=F32).astype(BF16).astype(F32)
        lo, hi = q[:, :half], q[:, half:]
        qf[:, i * head : i * head + half] = (lo * cos - hi * sin).astype(BF16).astype(F32)
        qf[:, i * head + half : (i + 1) * head] = (hi * cos + lo * sin).astype(BF16).astype(F32)
    start_k(SLOTS - 1)
    start_v(SLOTS - 1)
    hf[...] = xv[...].astype(F32)
    pl.semaphore_wait(barrier, n - 1)

    def score(s):
        row = qf[pl.ds(s, 1), :]
        which = lax.broadcasted_iota(jnp.int32, (8, head), 0)
        q = jnp.zeros((8, head), F32)
        for i in range(heads):
            q = jnp.where(which == i, row[:, i * head : (i + 1) * head], q)
        scores[rem(s, 2)] = lax.dot_general(
            q.astype(BF16), ks[rem(s, SLOTS)], (((1,), (1,)), ((), ())), preferred_element_type=F32
        )

    def soften(s):
        sc = scores[rem(s, 2)]
        e = jnp.exp((sc - jnp.max(sc, -1, keepdims=True)) * head**-0.5)
        probs[rem(s, 2)] = (e * (1.0 / jnp.sum(e, -1, keepdims=True))).astype(BF16)

    def gather(s):
        p, slot, hc = probs[rem(s, 2)], rem(s, SLOTS), cache // 2
        o = jnp.dot(p[:, :hc], vs[slot, :hc], preferred_element_type=F32)
        o = o + jnp.dot(p[:, hc:], vs[slot, hc:], preferred_element_type=F32)
        for i in range(heads):
            seen[pl.ds(rem(s, few), 1), i * head : (i + 1) * head] = o[i : i + 1]

    def term_copy(c, j):
        return remote(terms.at[0, c], terms.at[j, c], t_send.at[c, j], t_recv.at[c, j], peer(j))

    def send_terms(c):
        terms[0, c] = jnp.dot(seen[...].astype(BF16), wov[...], preferred_element_type=F32)[:few].astype(BF16)
        for j in range(1, n):
            term_copy(c, j).start()

    def take_terms(g):
        totals = []
        for i in range(group):
            c = g * group + i
            for j in range(1, n):
                term_copy(c, j).wait_recv()
            total = terms[lax.rem(me, n), c].astype(F32)
            for r in range(1, n):
                total = total + terms[lax.rem(me - r + n, n), c].astype(F32)
            totals.append(total)
        at_rows = tile_at(g, block)
        h = (hf[at_rows, :] + jnp.concatenate(totals, 0)).astype(BF16).astype(F32)
        hf[at_rows, :] = h
        bf[at_rows, :] = normed(h, gmv[...].astype(F32).reshape(1, d))

    kv_wait(k_ref, ks, k_sem, 0)
    score(0)
    start_k(SLOTS)
    kv_wait(k_ref, ks, k_sem, 1)
    score(1)
    start_k(SLOTS + 1)
    soften(0)
    first_spare = rows - 1 - SLOTS

    def step(s, _):
        kv_wait(k_ref, ks, k_sem, rem(s + 1, SLOTS))
        kv_wait(v_ref, vs, v_sem, rem(s - 1, SLOTS))
        gather(s - 1)
        soften(s)
        score(s + 1)

        @pl.when(s + 1 + SLOTS < rows)
        def _():
            start_k(s + 1 + SLOTS)

        @pl.when(s - 1 + SLOTS < rows)
        def _():
            start_v(s - 1 + SLOTS)

        for i in range(SLOTS):

            @pl.when(s == first_spare + i)
            def _():
                for c in weights_in[i * 3 : i * 3 + 3]:
                    c.start()

        @pl.when(lax.rem(s, few) == 0)
        def _():
            c = s // few - 1

            @pl.when(c == 0)
            def _():
                wo_in.wait()

            send_terms(c)
            g = s // block - 1

            @pl.when((lax.rem(s, block) == 0) & (g > 0))
            def _():
                take_terms(g - 1)

        return 0

    lax.fori_loop(1, rows - 1, step, 0)
    for c in weights_in[3 * SLOTS :]:
        c.start()
    kv_wait(v_ref, vs, v_sem, (rows - 2) % SLOTS)
    soften(rows - 1)
    gather(rows - 2)
    kv_wait(v_ref, vs, v_sem, (rows - 1) % SLOTS)
    gather(rows - 1)
    last = rows // few - 1
    send_terms(last)
    take_terms(n - 2)
    take_terms(n - 1)

    b16[...] = bf[...].astype(BF16)

    def hidden(j, _):
        pltpu.make_async_copy(wg_ref.at[:, pl.ds(0, gt)], wgv.at[j], g_sem.at[j]).wait()
        pltpu.make_async_copy(wu_ref.at[:, pl.ds(0, gt)], wuv.at[j], u_sem.at[j]).wait()
        gate = jnp.dot(b16[...], wgv[j], preferred_element_type=F32)
        up = jnp.dot(b16[...], wuv[j], preferred_element_type=F32)
        hid[:, tile_at(j, gt)] = (jax.nn.silu(gate) * up).astype(BF16)
        return 0

    lax.fori_loop(0, ng, hidden, 0)

    def a_copy(t):
        return remote(out16.at[t, 1 - core], pair.at[t], a_send.at[t], a_recv.at[t], partner)

    def m_copy(t, j):
        to = chip_at(j)
        return remote(mid.at[t, to], sums.at[j, t], m_send.at[t, j], m_recv.at[t, j], 2 * to + core)

    def y_at(t, dev):
        return y_ref.at[tile_at(dev, block), tile_at(t, dt)]

    def y_copy(t, j):
        mine = y_at(t, me)
        return remote(mine, mine, y_send.at[t, j], y_recv.at[t, j], partner if j == 0 else 2 * chip_at(j) + core)

    def f_copy(t, j):
        theirs = y_at(t, 2 * chip_at(chips - j) + core)
        return remote(theirs, theirs, f_send.at[t, j], f_recv.at[t, j], partner)

    def multiply(t):
        pltpu.make_async_copy(wd_ref.at[:, pl.ds(0, dt)], wdv.at[t], d_sem.at[t]).wait()
        out = jnp.dot(hid[...], wdv[t], preferred_element_type=F32)
        outf[t] = out
        out = out.astype(BF16)
        for i in range(n):
            out16[t, i % 2, i // 2] = out[i * block : (i + 1) * block]
        a_copy(t).start()

    def add_pair(t):
        a_copy(t).wait_recv()
        for j in range(1, chips):
            to = chip_at(j)
            mid[t, to] = (outf[t, tile_at(2 * to + core, block), :] + pair[t, to].astype(F32)).astype(BF16)
        for j in range(1, chips):
            m_copy(t, j).start()

    def finish(t):
        total = outf[t, tile_at(me, block), :] + pair[t, chip].astype(F32)
        for j in range(1, chips):
            m_copy(t, j).wait_recv()
        for j in range(1, chips):
            total = total + sums[j, t].astype(F32)
        y_ref[tile_at(me, block), tile_at(t, dt)] = (hf[tile_at(me, block), tile_at(t, dt)] + total).astype(BF16)
        for j in range(chips):
            y_copy(t, j).start()

    def forward(t):
        for j in range(1, chips):
            y_copy(t, j).wait_recv()
            f_copy(t, j).start()

    def down(u, _):
        pl.when(u < nd)(lambda: multiply(u))
        for lag, then in ((1, add_pair), (LAG, finish), (2 * LAG, forward)):
            pl.when((u >= lag) & (u < nd + lag))(lambda: then(u - lag))
        return 0

    lax.fori_loop(0, nd + 2 * LAG, down, 0)

    def drain_y(t, _):
        a_copy(t).wait_send()
        for j in range(chips):
            y_copy(t, j).wait_send()
        y_copy(t, 0).wait_recv()
        for j in range(1, chips):
            m_copy(t, j).wait_send()
            f_copy(t, j).wait_send()
            f_copy(t, j).wait_recv()
        return 0

    def drain_t(c, _):
        for j in range(1, n):
            term_copy(c, j).wait_send()
        return 0

    lax.fori_loop(0, last + 1, drain_t, 0)
    lax.fori_loop(0, nd, drain_y, 0)


def solution(mesh):
    n = mesh.shape["tp"]

    def step(x, k_cache, v_cache, gain_a, wq, wo, gain_m, w_gate, w_up, w_down):
        rows, d = x.shape
        cache, _, head = k_cache.shape[1:]
        half = head // 2
        angle = F32(cache - 1) * THETA ** (-jnp.arange(half, dtype=F32)[None] / half)
        block = rows // n
        chunks = rows // FEW
        ff = w_gate.shape[1]
        ng, nd = ff // HIDDEN_TILE, d // OUT_TILE
        k, v = (c.reshape(rows, cache, head) for c in (k_cache, v_cache))
        dma = pltpu.SemaphoreType.DMA
        return pl.pallas_call(
            functools.partial(layer, n),
            out_shape=jax.ShapeDtypeStruct((rows, d), BF16),
            in_specs=[pl.BlockSpec(memory_space=pl.ANY)] * 12,
            out_specs=pl.BlockSpec(memory_space=pltpu.VMEM),
            scratch_shapes=[
                pltpu.VMEM((rows, d), BF16),
                pltpu.VMEM((d,), BF16),
                pltpu.VMEM((d,), BF16),
                pltpu.VMEM((1, half), F32),
                pltpu.VMEM((1, half), F32),
                pltpu.VMEM((SLOTS, cache, head), BF16),
                pltpu.VMEM((SLOTS, cache, head), BF16),
                pltpu.VMEM(wo.shape, BF16),
                pltpu.VMEM((ng, d, HIDDEN_TILE), BF16),
                pltpu.VMEM((ng, d, HIDDEN_TILE), BF16),
                pltpu.VMEM((nd, ff, OUT_TILE), BF16),
                pltpu.VMEM((rows, wq.shape[1]), F32),
                pltpu.VMEM((2, 8, cache), F32),
                pltpu.VMEM((2, 8, cache), BF16),
                pltpu.VMEM((8, wq.shape[1]), F32),
                pltpu.VMEM((n, chunks, FEW, d), BF16),
                pltpu.VMEM((rows, d), F32),
                pltpu.VMEM((rows, d), F32),
                pltpu.VMEM((rows, d), BF16),
                pltpu.VMEM((rows, ff), BF16),
                pltpu.VMEM((nd, rows, OUT_TILE), F32),
                pltpu.VMEM((nd, 2, n // 2, block, OUT_TILE), BF16),
                pltpu.VMEM((nd, n // 2, block, OUT_TILE), BF16),
                pltpu.VMEM((nd, n // 2, block, OUT_TILE), BF16),
                pltpu.VMEM((n // 2, nd, block, OUT_TILE), BF16),
                dma((5,)),
                dma((SLOTS,)),
                dma((SLOTS,)),
                dma((2,)),
                dma,
                dma((ng,)),
                dma((ng,)),
                dma((nd,)),
                dma((chunks, n)),
                dma((chunks, n)),
                dma((nd,)),
                dma((nd,)),
                dma((nd, n // 2)),
                dma((nd, n // 2)),
                dma((nd, n // 2)),
                dma((nd, n // 2)),
                dma((nd, n // 2)),
                dma((nd, n // 2)),
            ],
            compiler_params=pltpu.CompilerParams(collective_id=0, has_side_effects=True, vmem_limit_bytes=VMEM_LIMIT),
        )(x, k, v, gain_a, wq, wo, gain_m, w_gate, w_up, w_down, jnp.cos(angle), jnp.sin(angle))

    states, cache, columns, rows_of = P("dp", None), P("dp", None, "tp", None), P(None, "tp"), P("tp", None)
    return jax.shard_map(
        step,
        mesh=mesh,
        in_specs=(states, cache, cache, P(None), columns, rows_of, P(None), columns, columns, rows_of),
        out_specs=states,
        check_vma=False,
    )
```

time: 166 us -> 121 us (0.73)
  Pallas kernels: 160 us -> 118 us
  local copies, waits for them, and re-layouts: 4.42 us -> 1.82 us
    pallas_call x1, Pallas kernels: 160 us -> 118 us  [step(): pl.pallas_call(functools.partial(layer, n), out_shape=jax.ShapeDtypeStruc...]
    reshape x2 -> x0, local copies, waits for them, and re-layouts: 2.61 us -> none  [the longest x1 1.3 us: step(): gain_a.reshape(1, d)]
where the time goes in v2:
time: 121 us
  Pallas kernels  118 us (98%)
  local copies, waits for them, and re-layouts  1.82 us (2%)
    pallas_call x1, Pallas kernels, step(): pl.pallas_call(functools.partial(layer, n), out_shape=jax.ShapeDtypeStruc...  118 us

profile of v2, /device:TPU:113, one launch (start us, length us, event | category | flops | bytes accessed | tf_op | source)
XLA Modules:
  0.0 120.7 jit_solution(311874221473646511)
XLA Ops:
  0.0 0.7 fusion
  0.7 118.3 %shard_map.100 = bf16[64,3584]{1,0:T(8,128)(2,1)} custom-call(bf16[64,3584]{1,0:T(8,128)(2,1)} %x_ref.1, bf16[64,4096,256]{2,1,0:T(8,128)(2,1)} %bitcast.k_ref, bf16[64,4096,256]{2,1,0:T(8,128)(2,1)} %bitcast.1.v_ref, bf16[3584]{0:T(1024)(128)(2,1)} %ga_ref.1, bf16[3584,512]{1,0:T(8,128)(2,1)} %wq_ref.1, bf16[512,3584]{1,0:T(8,128)(2,1)} %wo_ref.1, ...), custom_call_target="tpu_custom_call" | custom-call | tf_op jit(solution)/shard_map/pallas_call | solution.py:329
  118.9 1.8 %copy.12 = bf16[64,3584]{1,0:T(8,128)(2,1)} copy(bf16[64,3584]{1,0:T(8,128)(2,1)} %shard_map.100) | data formatting | bytes 917504

commit v3 on v2

--- a/solution.py
+++ b/solution.py
@@ -14,7 +14,9 @@
 HIDDEN_TILE = 256
 OUT_TILE = 512
 FEW = 4
-LAG = 4
+LAG = 3
+AHEAD = 6
+EARLY = 8
 VMEM_LIMIT = 66_000_000
 F32 = jnp.float32
 BF16 = jnp.bfloat16
@@ -189,8 +191,7 @@
 
             @pl.when(s == first_spare + i)
             def _():
-                for c in weights_in[i * 3 : i * 3 + 3]:
-                    c.start()
+                weights_in[i].start()
 
         @pl.when(lax.rem(s, few) == 0)
         def _():
@@ -210,29 +211,45 @@
         return 0
 
     lax.fori_loop(1, rows - 1, step, 0)
-    for c in weights_in[3 * SLOTS :]:
+    for c in weights_in[SLOTS : SLOTS + 2]:
         c.start()
     kv_wait(v_ref, vs, v_sem, (rows - 2) % SLOTS)
     soften(rows - 1)
     gather(rows - 2)
+    for c in weights_in[SLOTS + 2 : AHEAD]:
+        c.start()
     kv_wait(v_ref, vs, v_sem, (rows - 1) % SLOTS)
     gather(rows - 1)
     last = rows // few - 1
     send_terms(last)
     take_terms(n - 2)
+    for i in range(EARLY):
+        weights_in[i].wait()
+        weights_in[i + AHEAD].start()
     take_terms(n - 1)
 
     b16[...] = bf[...].astype(BF16)
 
+    def start_down(t):
+        pltpu.make_async_copy(wd_ref.at[:, tile_at(t, dt)], wdv.at[t], d_sem.at[t]).start()
+
     def hidden(j, _):
-        pltpu.make_async_copy(wg_ref.at[:, pl.ds(0, gt)], wgv.at[j], g_sem.at[j]).wait()
-        pltpu.make_async_copy(wu_ref.at[:, pl.ds(0, gt)], wuv.at[j], u_sem.at[j]).wait()
+        @pl.when(j >= EARLY // 2)
+        def _():
+            pltpu.make_async_copy(wg_ref.at[:, pl.ds(0, gt)], wgv.at[j], g_sem.at[j]).wait()
+            pltpu.make_async_copy(wu_ref.at[:, pl.ds(0, gt)], wuv.at[j], u_sem.at[j]).wait()
+            start_down(2 * (j - EARLY // 2))
+            start_down(2 * (j - EARLY // 2) + 1)
+
         gate = jnp.dot(b16[...], wgv[j], preferred_element_type=F32)
         up = jnp.dot(b16[...], wuv[j], preferred_element_type=F32)
         hid[:, tile_at(j, gt)] = (jax.nn.silu(gate) * up).astype(BF16)
         return 0
 
+    assert EARLY + AHEAD == 2 * ng and nd <= 2 * ng
     lax.fori_loop(0, ng, hidden, 0)
+    for t in range(AHEAD, nd):
+        start_down(t)
 
     def a_copy(t):
         return remote(out16.at[t, 1 - core], pair.at[t], a_send.at[t], a_recv.at[t], partner)
@@ -286,11 +303,11 @@
 
     def down(u, _):
         pl.when(u < nd)(lambda: multiply(u))
-        for lag, then in ((1, add_pair), (LAG, finish), (2 * LAG, forward)):
+        for lag, then in ((LAG, add_pair), (nd + LAG, finish), (2 * nd + LAG, forward)):
             pl.when((u >= lag) & (u < nd + lag))(lambda: then(u - lag))
         return 0
 
-    lax.fori_loop(0, nd + 2 * LAG, down, 0)
+    lax.fori_loop(0, 3 * nd + LAG, down, 0)
 
     def drain_y(t, _):
         a_copy(t).wait_send()
@@ -328,7 +345,7 @@
         dma = pltpu.SemaphoreType.DMA
         return pl.pallas_call(
             functools.partial(layer, n),
-            out_shape=jax.ShapeDtypeStruct((rows, d), BF16),
+            out_shape=pltpu.VMEM((rows, d), BF16),
             in_specs=[pl.BlockSpec(memory_space=pl.ANY)] * 12,
             out_specs=pl.BlockSpec(memory_space=pltpu.VMEM),
             scratch_shapes=[

time: 121 us -> 114 us (0.942)
  Pallas kernels: 118 us -> 113 us
    pallas_call x1, Pallas kernels: 118 us -> 113 us  [step(): pl.pallas_call(functools.partial(layer, n), out_shape=pltpu.VMEM((rows, d...]
where the time goes in v3:
time: 114 us
  Pallas kernels  113 us (99%)
    pallas_call x1, Pallas kernels, step(): pl.pallas_call(functools.partial(layer, n), out_shape=pltpu.VMEM((rows, d...  113 us

profile of v3, /device:TPU:113, one launch (start us, length us, event | category | flops | bytes accessed | tf_op | source)
XLA Modules:
  0.0 114.3 jit_solution(16117821858178556013)
XLA Ops:
  0.0 0.6 fusion
  0.6 112.9 %shard_map.100 = bf16[64,3584]{1,0:T(8,128)(2,1)S(1)} custom-call(bf16[64,3584]{1,0:T(8,128)(2,1)} %x_ref.1, bf16[64,4096,256]{2,1,0:T(8,128)(2,1)} %bitcast.k_ref, bf16[64,4096,256]{2,1,0:T(8,128)(2,1)} %bitcast.1.v_ref, bf16[3584]{0:T(1024)(128)(2,1)} %ga_ref.1, bf16[3584,512]{1,0:T(8,128)(2,1)} %wq_ref.1, bf16[512,3584]{1,0:T(8,128)(2,1)} %wo_ref.1, ...), custom_call_target="tpu_custom_call" | custom-call | tf_op jit(solution)/shard_map/pallas_call | solution.py:346
  113.5 0.8 copy.12
